TPU v7x, 32 devices: a whole 2x2x4 slice. The times are simulated.
32 devices in a mesh: batch: 16 (over z, y, core), rep: 2 (over x).
Axes of the slice: x: 2, y: 2, z: 4, core: 2. Of those that a mesh axis runs over, the one named last changes fastest.
Arguments:
- image_embed: bfloat16 [2048, 1024], P('batch'), may hold values from -2 to 2
- text_embed: bfloat16 [2048, 1024], P(('batch', 'rep')), may hold values from -2 to 2
- logit_scale: float32 [1], replicated, may hold values from 50 to 100
Outputs:
- mean_loss: float32 [], replicated
- image_grad: float32 [2048, 1024], P(('batch', 'rep'))
- text_grad: float32 [2048, 1024], P(('batch', 'rep'))
All inputs are finite; a program needn't handle non-finite values.
Results may differ from a plain program's by a relative error of at most 0.0025.
Values may be sent and summed in bfloat16 or wider, within the bound.
A program may use at most 128 MiB of HBM per device.

v0:
```python
import jax
import jax.numpy as jnp
from jax import lax
from jax.sharding import PartitionSpec as P


def merged(value, axis, join):
    pieces = jax.tree.map(lambda part: lax.all_gather(part, axis), value)
    head = jax.tree.map(lambda part: part[0], pieces)
    tail = jax.tree.map(lambda part: part[1:], pieces)
    total, _ = lax.scan(lambda total, share: (join(total, share), None), head, tail)
    return total


def combine_lse(earlier, later):
    biggest = jnp.maximum(earlier[0], later[0])
    return (
        biggest,
        earlier[1] * jnp.exp(earlier[0] - biggest) + later[1] * jnp.exp(later[0] - biggest),
    )


def body(image_embed, text_embed, logit_scale):
    scale_value = logit_scale[0]
    row_count = image_embed.shape[0]
    half_rows = text_embed.shape[0]
    batch_count = lax.axis_size("batch")
    batch_index = lax.axis_index("batch")
    rep_index = lax.axis_index("rep")
    whole_text = lax.all_gather(text_embed, "batch", axis=0, tiled=True)
    scores = scale_value * lax.dot_general(
        image_embed, whole_text, (((1,), (1,)), ((), ())), preferred_element_type=jnp.float32
    )
    row_max = jnp.max(scores, axis=1)
    row_sum = jnp.sum(jnp.exp(scores - row_max[:, None]), axis=1)
    row_max, row_sum = merged((row_max, row_sum), "rep", combine_lse)
    row_lse = row_max + jnp.log(row_sum)
    column_max = jnp.max(scores, axis=0)
    column_sum = jnp.sum(jnp.exp(scores - column_max[None, :]), axis=0)
    peer_maxes, peer_sums = (
        lax.all_to_all(
            column_max.reshape(batch_count, half_rows),
            "batch",
            split_axis=0,
            concat_axis=0,
            tiled=True,
        ),
        lax.all_to_all(
            column_sum.reshape(batch_count, half_rows),
            "batch",
            split_axis=0,
            concat_axis=0,
            tiled=True,
        ),
    )
    column_top = jnp.max(peer_maxes, axis=0)
    own_lse = column_top + jnp.log(
        jnp.sum(peer_sums * jnp.exp(peer_maxes - column_top[None, :]), axis=0)
    )
    col_lse = lax.all_gather(own_lse, "batch", axis=0, tiled=True)
    own_scores = lax.dynamic_slice(
        scores, (rep_index * half_rows, batch_index * half_rows), (half_rows, half_rows)
    )
    own_diag = jnp.diagonal(own_scores)
    own_rows = lax.dynamic_slice_in_dim(row_lse, rep_index * half_rows, half_rows, 0)
    loss_sum = lax.psum(jnp.sum(own_rows + own_lse - 2.0 * own_diag), ("batch", "rep"))
    mean_loss = loss_sum / (2 * row_count * batch_count)
    row_ids = lax.broadcasted_iota(jnp.int32, scores.shape, 0) - rep_index * half_rows
    column_ids = lax.broadcasted_iota(jnp.int32, scores.shape, 1) - batch_index * half_rows
    diag_match = ((row_ids == column_ids) & (column_ids >= 0) & (column_ids < half_rows)).astype(
        jnp.float32
    )
    weights = (
        jnp.exp(scores - row_lse[:, None]) + jnp.exp(scores - col_lse[None, :]) - 2.0 * diag_match
    ).astype(jnp.bfloat16)
    image_part = (
        scale_value * 0.5 * jnp.dot(weights, whole_text, preferred_element_type=jnp.float32)
    )
    image_grad = lax.psum_scatter(image_part, "rep", scatter_dimension=0, tiled=True)
    all_rows_lse = lax.all_gather(row_lse, "batch", axis=0, tiled=True)
    own_first = (2 * batch_index + rep_index) * half_rows
    fragment = lax.all_gather(image_embed, "batch", axis=0, tiled=True)
    scores_back = scale_value * lax.dot_general(
        text_embed, fragment, (((1,), (1,)), ((), ())), preferred_element_type=jnp.float32
    )
    image_ids = lax.broadcasted_iota(jnp.int32, scores_back.shape, 1)
    text_ids = own_first + lax.broadcasted_iota(jnp.int32, scores_back.shape, 0)
    back_match = (image_ids == text_ids).astype(jnp.float32)
    weights_block = (
        jnp.exp(scores_back - own_lse[:, None])
        + jnp.exp(scores_back - all_rows_lse[None, :])
        - 2.0 * back_match
    ).astype(jnp.bfloat16)
    summed = jnp.dot(weights_block, fragment, preferred_element_type=jnp.float32)
    text_grad = scale_value * 0.5 * summed
    return (mean_loss, image_grad, text_grad)


def solution(mesh):
    in_specs = (P("batch", None), P(("batch", "rep"), None), P())
    out_specs = (P(), P(("batch", "rep"), None), P(("batch", "rep"), None))
    return jax.shard_map(body, mesh=mesh, in_specs=in_specs, out_specs=out_specs, check_vma=False)
```

profile of v0, /device:TPU:0, one launch (start us, length us, event | category | flops | bytes accessed | tf_op | source)
XLA Modules:
  0.0 188.3 jit_solution(3406999537041525352)
XLA Ops:
  7.2 0.0 all-gather.8.cloned.1.call-start
  7.2 0.7 all-gather.8.cloned.1.call-update
  7.9 0.0 copy-start
  7.9 0.0 all-gather.10.cloned.1.call-start
  8.0 0.7 all-gather.10.cloned.1.call-update
  9.3 1.2 dynamic-slice
  11.2 43.1 %all-gather.8.cloned.1.call-done = bf16[1024,1024]{1,0:T(8,128)(2,1)} async-done(((bf16[64,1024]{1,0:T(8,128)(2,1)}), bf16[1024,1024]{1,0:T(8,128)(2,1)}) %all-gather.8.cloned.1.call-update) | async-done | bytes 2097168 | tf_op jit(solution)/shard_map/all_gather | solution.py:30
  54.3 2.6 %fusion.24 = (f32[128]{0:T(128)S(1)}, f32[1024]{0:T(1024)S(1)}, f32[128,1024]{1,0:T(8,128)S(1)}) fusion(bf16[128,1024]{1,0:T(8,128)(2,1)} %param.3, bf16[1024,1024]{1,0:T(8,128)(2,1)} %all-gather.8.cloned.1.call-done, f32[]{:T(128)} %bitcast.40), kind=kOutput, calls=%fused_computation.47 | convolution fusion | flops 268827520 | bytes 2888196 | tf_op jit(solution)/shard_map/dot_general | solution.py:31
  57.0 0.7 all_to_all.16
  57.6 3.5 %all-to-all-start = ((f32[16,1,64]{2,1,0:T(1,128)}), f32[16,1,64]{2,1,0:T(1,128)S(1)}, u32[]{:S(2)}, u32[]{:S(2)}) async-start(f32[16,1,64]{2,1,0:T(1,128)} %all_to_all.16), calls=%async_computation | async-start | bytes 16384 | tf_op jit(solution)/shard_map/all_to_all | solution.py:41
  61.1 0.2 exponential_reduce_fusion.1
  61.4 0.7 all_to_all.18
  62.0 4.2 %all-gather.3 = f32[2,1,128]{2,1,0:T(1,128)S(1)} all-gather(f32[1,1,128]{2,1,0:T(1,128)S(1)} %bitcast.48), channel_id=3, replica_groups=mesh['batch'=16,'rep'=2] {'rep'}, dimensions={0}, use_global_device_ids=true | all-gather | bytes 1536 | tf_op jit(solution)/shard_map/all_gather | solution.py:8
  66.3 4.2 %all-gather.2 = f32[2,1,128]{2,1,0:T(1,128)S(1)} all-gather(f32[1,1,128]{2,1,0:T(1,128)S(1)} %bitcast.47), channel_id=2, replica_groups=mesh['batch'=16,'rep'=2] {'rep'}, dimensions={0}, use_global_device_ids=true | all-gather | bytes 1536 | tf_op jit(solution)/shard_map/all_gather | solution.py:8
  70.5 0.0 all-to-all-done
  70.5 6.0 %all-to-all-start.1 = ((f32[16,1,64]{2,1,0:T(1,128)}), f32[16,1,64]{2,1,0:T(1,128)S(1)}, u32[]{:S(2)}, u32[]{:S(2)}) async-start(f32[16,1,64]{2,1,0:T(1,128)} %all_to_all.18), calls=%async_computation.1 | async-start | bytes 16384 | tf_op jit(solution)/shard_map/all_to_all | solution.py:48
  76.5 0.0 reduce-scatter.2.cloned.1.call-start
  76.6 6.3 %all-to-all-done.1 = f32[16,1,64]{2,1,0:T(1,128)S(1)} async-done(((f32[16,1,64]{2,1,0:T(1,128)}), f32[16,1,64]{2,1,0:T(1,128)S(1)}, u32[]{:S(2)}, u32[]{:S(2)}) %all-to-all-start.1) | async-done | bytes 4128 | tf_op jit(solution)/shard_map/all_to_all | solution.py:48
  82.9 0.1 fusion.25
  83.0 30.3 %all-reduce = f32[1024]{0:T(1024)S(1)} all-reduce(f32[1024]{0:T(1024)S(1)} %get-tuple-element.22), channel_id=1, replica_groups=mesh['batch'=16,'rep'=2] {'batch'}, use_global_device_ids=true, to_apply=%add | all-reduce | flops 1024 | bytes 8192
  113.3 3.0 %convolution_multiply_fusion.1 = f32[128,1024]{1,0:T(8,128)} fusion(bf16[1024,1024]{1,0:T(8,128)(2,1)} %all-gather.8.cloned.1.call-done, f32[128,1024]{1,0:T(8,128)S(1)} %get-tuple-element.24, s32[1024]{0:T(1024)S(1)} %iota_subtract_fusion, f32[1024]{0:T(1024)S(1)} %all-reduce, f32[128]{0:T(128)S(1)} %log_add_fusion.1, f32[]{:T(128)S(6)} %mul.86, ...), kind=kOutput, calls=%fused_computation.2 | convolution fusion | flops 269746176 | bytes 3156996 | tf_op jit(solution)/shard_map/dot_general | solution.py:77
  116.3 0.0 reduce-scatter.2.cloned.1.call-update
  116.4 0.1 dynamic_slice.12
  116.5 0.8 gather_fusion
  117.3 0.7 subtract_reduce_fusion
  118.0 17.1 %all-gather.4 = f32[16,1,128]{2,1,0:T(1,128)S(1)} all-gather(f32[1,1,128]{2,1,0:T(1,128)S(1)} %bitcast.46), channel_id=1, replica_groups=mesh['batch'=16,'rep'=2] {'batch'}, dimensions={0}, use_global_device_ids=true | all-gather | bytes 8704 | tf_op jit(solution)/shard_map/all_gather | solution.py:80
  135.1 38.4 %psum.7 = f32[]{:T(128)} all-reduce(f32[]{:T(128)} %subtract_reduce_fusion), channel_id=1, replica_groups=mesh['batch'=16,'rep'=2] {'batch','rep'}, use_global_device_ids=true, to_apply=%region_7.8 | all-reduce | flops 1 | bytes 8 | tf_op jit(solution)/shard_map/psum | solution.py:66
  174.2 0.0 all-gather.10.cloned.1.call-done
  174.2 0.0 copy-done
  174.2 6.4 %convolution_multiply_fusion.3 = f32[64,1024]{1,0:T(8,128)} fusion(bf16[2048,1024]{1,0:T(8,128)(2,1)} %all-gather.10.cloned.1.call-done, bf16[64,1024]{1,0:T(8,128)(2,1)S(1)} %copy-done, s32[64]{0:T(128)S(1)} %iota_add_fusion, f32[2048]{0:T(1024)S(1)} %bitcast.45, f32[64]{0:T(128)S(1)} %get-tuple-element.23, f32[]{:T(128)} %bitcast.42, f32[]{:T(128)S(6)} %mul.86), kind=kOutput, calls=%fused_computation.4 | convolution fusion | flops 537985024 | bytes 4596232 | tf_op jit(solution)/shard_map/dot_general | solution.py:94
  180.6 0.0 reduce-scatter.2.cloned.1.call-done
  (9 shorter events, 0.1 us)
Async XLA Ops:
  7.2 47.2 %all-gather.8.cloned.1.call-start = ((), (), s32[]{:S(2)}) async-start(), calls=%async_computation.3 | async-start | bytes 2228224 | tf_op jit(solution)/shard_map/all_gather | solution.py:30
  7.9 166.3 %copy-start = (bf16[64,1024]{1,0:T(8,128)(2,1)S(1)}, bf16[64,1024]{1,0:T(8,128)(2,1)}, u32[]{:S(2)}) copy-start(bf16[64,1024]{1,0:T(8,128)(2,1)} %param.4) | copy-start | bytes 393220
  7.9 166.3 %all-gather.10.cloned.1.call-start = ((), (), s32[]{:S(2)}) async-start(), calls=%async_computation.5 | async-start | bytes 4456448 | tf_op jit(solution)/shard_map/all_gather | solution.py:82
  57.6 12.9 %all-to-all-start = ((f32[16,1,64]{2,1,0:T(1,128)}), f32[16,1,64]{2,1,0:T(1,128)S(1)}, u32[]{:S(2)}, u32[]{:S(2)}) async-start(f32[16,1,64]{2,1,0:T(1,128)} %all_to_all.16), calls=%async_computation | async-start | bytes 16384 | tf_op jit(solution)/shard_map/all_to_all | solution.py:41
  70.5 12.3 %all-to-all-start.1 = ((f32[16,1,64]{2,1,0:T(1,128)}), f32[16,1,64]{2,1,0:T(1,128)S(1)}, u32[]{:S(2)}, u32[]{:S(2)}) async-start(f32[16,1,64]{2,1,0:T(1,128)} %all_to_all.18), calls=%async_computation.1 | async-start | bytes 16384 | tf_op jit(solution)/shard_map/all_to_all | solution.py:48
  76.5 104.1 %reduce-scatter.2.cloned.1.call-start = ((), (), s32[]{:S(2)}) async-start(), calls=%async_computation.4 | async-start | bytes 786432 | tf_op jit(solution)/shard_map/reduce_scatter | solution.py:79
Sparse Core Ops, SparseCore 0:
  10.1 44.1 all-gather.7
  56.5 49.5 all-gather.9
  116.5 11.8 reduce-scatter.1
where the time goes:
time: 189 us; the launch traced here: 188 us
  blocking collectives  94.3 us (50%)
  waiting for transfers between devices  50.8 us (27%)
  between operations  16.9 us (9%)
  matrix products  12 us (6%)
  starting transfers between devices  9.56 us (5%)
  local copies, waits for them, and re-layouts  3.51 us (2%)
    all_gather x1, waiting for transfers between devices, body(): whole_text = lax.all_gather(text_embed, 'batch', axis=0, tiled=True)  43.1 us
    psum x1, blocking collectives, body(): lax.psum(jnp.sum(own_rows + own_lse - 2.0 * own_diag), ('batch', 'rep'))  38.4 us
    unnamed x1, blocking collectives  30.3 us
    all_gather x1, blocking collectives, body(): all_rows_lse = lax.all_gather(row_lse, 'batch', axis=0, tiled=True)  17.1 us
    all_gather x2, blocking collectives, merged(): pieces = jax.tree.map(lambda part: lax.all_gather(part, axis), value)  8.45 us
    dot_general x1, matrix products, body(): jnp.dot(weights_block, fragment, preferred_element_type=jnp.float32)  6.37 us
    all_to_all x1, waiting for transfers between devices, body(): lax.all_to_all(column_sum.reshape(batch_count, half_rows), 'batch', split...  6.25 us
    all_to_all x1, starting transfers between devices, body(): lax.all_to_all(column_sum.reshape(batch_count, half_rows), 'batch', split...  5.97 us
  transfers between devices with their start and end apart: 5, of which 2 were waited for; matrix products, arithmetic and copies ran while one was open for 8% of the time, Pallas kernels for 0%

commit v1 on v0

v1 whole, which is shorter than its diff:
```python
import functools

import jax
import jax.numpy as jnp
from jax import lax
from jax.experimental import pallas as pl
from jax.experimental.pallas import tpu as pltpu
from jax.sharding import PartitionSpec as P

MESH = pl.DeviceIdType.MESH
F32 = jnp.float32
BF16 = jnp.bfloat16


def nt_dot(a, b):
    return lax.dot_general(a, b, (((1,), (1,)), ((), ())), preferred_element_type=F32)


def tn_dot(a, b):
    return lax.dot_general(a, b, (((0,), (0,)), ((), ())), preferred_element_type=F32)


def kernel(
    low_count,
    high_count,
    pair_count,
    scale_ref,
    image_hbm,
    text_hbm,
    loss_ref,
    image_grad_ref,
    text_grad_ref,
    images,
    texts,
    scores,
    weights,
    row_stats,
    column_stats,
    row_loss,
    column_loss,
    image_out,
    text_out,
    image_in,
    text_in,
    image_own,
    text_own,
    local_sems,
    image_send,
    image_recv,
    text_send,
    text_recv,
    row_send,
    row_recv,
    column_send,
    column_recv,
    row_loss_send,
    row_loss_recv,
    column_loss_send,
    column_loss_recv,
    image_out_send,
    image_out_recv,
    text_out_send,
    text_out_recv,
):
    rows = images.shape[1]
    half = rows // 2
    columns = texts.shape[0]
    batch = lax.axis_index("batch")
    rep = lax.axis_index("rep")
    high = batch // low_count
    low = lax.rem(batch, low_count)
    member = low * 2 + rep
    member_count = 2 * low_count
    scale = scale_ref[0]

    def row_device(index):
        return (high * low_count + index // 2, jnp.int32(index % 2))

    def column_device(index):
        return (index * low_count + low, rep)

    own_text = pl.ds(pl.multiple_of(high * half, half), half)
    image_load = pltpu.make_async_copy(image_hbm, images.at[low], local_sems.at[0])
    text_load = pltpu.make_async_copy(text_hbm, texts.at[own_text], local_sems.at[1])
    image_load.start()
    text_load.start()

    barrier = pltpu.get_barrier_semaphore()
    for index in range(member_count):

        @pl.when(index != member)
        def _():
            pl.semaphore_signal(barrier, inc=1, device_id=row_device(index), device_id_type=MESH)

    for index in range(high_count):

        @pl.when(index != high)
        def _():
            pl.semaphore_signal(barrier, inc=1, device_id=column_device(index), device_id_type=MESH)

    pl.semaphore_wait(barrier, member_count + high_count - 2)

    def remote(source, target, send, recv, device):
        return pltpu.make_async_remote_copy(
            src_ref=source,
            dst_ref=target,
            send_sem=send,
            recv_sem=recv,
            device_id=device,
            device_id_type=MESH,
        )

    def text_slot(index):
        return texts.at[pl.ds(index * half, half)]

    def image_copy(index):
        return remote(
            images.at[low], images.at[low], image_send.at[index], image_recv.at[low],
            (high * low_count + index, rep),
        )

    def text_copy(index):
        return remote(
            texts.at[own_text], texts.at[own_text], text_send.at[index], text_recv.at[high],
            column_device(index),
        )

    def slot_copy(buffer, slot, send, recv, index, device):
        return remote(buffer.at[slot], buffer.at[slot], send.at[index], recv.at[slot], device)

    def row_copy(index):
        return slot_copy(row_stats, member, row_send, row_recv, index, row_device(index))

    def column_copy(index):
        return slot_copy(column_stats, high, column_send, column_recv, index, column_device(index))

    def row_loss_copy(index):
        return slot_copy(row_loss, high, row_loss_send, row_loss_recv, index, column_device(index))

    def column_loss_copy(index):
        return slot_copy(
            column_loss, member, column_loss_send, column_loss_recv, index, row_device(index)
        )

    def image_out_copy(index):
        return remote(
            image_out.at[index], image_in.at[member], image_out_send.at[index],
            image_out_recv.at[member], row_device(index),
        )

    def text_out_copy(index):
        return remote(
            text_out.at[index], text_in.at[high], text_out_send.at[index],
            text_out_recv.at[high], column_device(index),
        )

    def arrived(buffer, recv, index):
        remote(buffer, buffer, recv.at[index], recv.at[index], (batch, rep)).wait_recv()

    def each(count, own, action):
        for index in range(count):

            @pl.when(index != own)
            def _():
                action(index)

    text_load.wait()
    each(high_count, high, lambda index: text_copy(index).start())
    image_load.wait()
    each(low_count, low, lambda index: image_copy(index).start())

    each(high_count, high, lambda index: arrived(text_slot(index), text_recv, index))

    diag_start = rep * half
    row_iota = lax.broadcasted_iota(jnp.int32, (rows, columns), 0)
    column_iota = lax.broadcasted_iota(jnp.int32, (rows, columns), 1) - high * half
    in_diag = (column_iota >= 0) & (column_iota < half)

    def diag_of(index):
        return in_diag & (row_iota - diag_start == column_iota) & (low == index)

    lanes = lax.broadcasted_iota(jnp.int32, (rows, 128), 1)
    column_max = None
    diag_sum = jnp.zeros((1, columns), F32)
    for index in range(low_count):

        @pl.when(index != low)
        def _():
            arrived(images.at[index], image_recv, index)

        block = scale * nt_dot(images[index], texts[...])
        scores[index] = block
        row_max = jnp.max(block, axis=1, keepdims=True)
        row_sum = jnp.sum(jnp.exp(block - row_max), axis=1, keepdims=True)
        packed = jnp.where(lanes == 0, row_max, row_sum).T
        row_stats[member, 0:2, index * rows : (index + 1) * rows] = packed[0:2]
        block_max = jnp.max(block, axis=0, keepdims=True)
        new_max = block_max if column_max is None else jnp.maximum(column_max, block_max)
        block_sum = jnp.sum(jnp.exp(block - new_max), axis=0, keepdims=True)
        if column_max is None:
            column_sum = block_sum
        else:
            column_sum = column_sum * jnp.exp(column_max - new_max) + block_sum
        column_max = new_max
        diag_sum = diag_sum + jnp.sum(
            jnp.where(diag_of(index), block, 0.0), axis=0, keepdims=True
        )
    row_stats[member, 2:3, :] = jnp.full((1, low_count * rows), jnp.sum(diag_sum), F32)
    column_stats[high, 0:1, :] = column_max
    column_stats[high, 1:2, :] = column_sum
    each(high_count, high, lambda index: column_copy(index).start())
    each(member_count, member, lambda index: row_copy(index).start())

    def merged(stats, count):
        top = stats[0, 0:1, :]
        for index in range(1, count):
            top = jnp.maximum(top, stats[index, 0:1, :])
        total = jnp.zeros_like(top)
        for index in range(count):
            total = total + stats[index, 1:2, :] * jnp.exp(stats[index, 0:1, :] - top)
        return top + jnp.log(total)

    each(member_count, member, lambda index: arrived(row_stats.at[index], row_recv, index))
    row_lse = merged(row_stats, member_count)
    each(high_count, high, lambda index: arrived(column_stats.at[index], column_recv, index))
    column_lse = merged(column_stats, high_count)

    diag_total = row_stats[0, 2:3, 0:128]
    for index in range(1, member_count):
        diag_total = diag_total + row_stats[index, 2:3, 0:128]
    row_loss[high] = jnp.full((1, 128), jnp.sum(row_lse), F32) - 2.0 * diag_total
    column_loss[member] = jnp.full((1, 128), jnp.sum(column_lse), F32)
    each(high_count, high, lambda index: row_loss_copy(index).start())
    each(member_count, member, lambda index: column_loss_copy(index).start())

    for index in range(low_count):
        span = pl.ds(index * rows, rows)
        block = scores[index]
        spread = jnp.broadcast_to(row_lse[:, index * rows : (index + 1) * rows], (128, rows)).T
        weights[span] = (
            jnp.exp(block - spread[:, 0:1])
            + jnp.exp(block - column_lse)
            - jnp.where(diag_of(index), 2.0, 0.0)
        ).astype(BF16)

    per_dot = 128 // half
    for start in range(0, high_count, per_dot):
        part = tn_dot(
            weights[:, start * half : (start + per_dot) * half],
            images[...].reshape(low_count * rows, images.shape[2]),
        )
        for offset in range(per_dot):
            index = start + offset
            piece = part[offset * half : (offset + 1) * half]
            text_out[index] = piece.astype(BF16)

            @pl.when(index != high)
            def _():
                text_out_copy(index).start()

            @pl.when(index == high)
            def _():
                text_own[...] = piece

    for low_index in range(low_count):
        part = jnp.dot(
            weights[pl.ds(low_index * rows, rows)], texts[...], preferred_element_type=F32
        )
        for offset in range(2):
            index = 2 * low_index + offset
            piece = part[offset * half : (offset + 1) * half]
            image_out[index] = piece.astype(BF16)

            @pl.when(index != member)
            def _():
                image_out_copy(index).start()

            @pl.when(index == member)
            def _():
                image_own[...] = piece

    each(high_count, high, lambda index: arrived(row_loss.at[index], row_loss_recv, index))
    each(
        member_count, member, lambda index: arrived(column_loss.at[index], column_loss_recv, index)
    )
    total = row_loss[0]
    for index in range(1, high_count):
        total = total + row_loss[index]
    for index in range(member_count):
        total = total + column_loss[index]
    loss_ref[0, 0] = jnp.max(total) / (2 * pair_count)

    factor = scale * 0.5
    each(high_count, high, lambda index: arrived(text_in.at[index], text_out_recv, index))
    total = text_own[...]
    for index in range(1, high_count):
        total = total + text_in[lax.rem(high + index, high_count)].astype(F32)
    text_grad_ref[...] = factor * total
    each(member_count, member, lambda index: arrived(image_in.at[index], image_out_recv, index))
    total = image_own[...]
    for index in range(1, member_count):
        total = total + image_in[lax.rem(member + index, member_count)].astype(F32)
    image_grad_ref[...] = factor * total

    for count, own, copy in (
        (low_count, low, image_copy),
        (high_count, high, text_copy),
        (member_count, member, row_copy),
        (high_count, high, column_copy),
        (high_count, high, row_loss_copy),
        (member_count, member, column_loss_copy),
        (member_count, member, image_out_copy),
        (high_count, high, text_out_copy),
    ):
        each(count, own, lambda index: copy(index).wait_send())


def body(image_embed, text_embed, logit_scale):
    rows, width = image_embed.shape
    half = text_embed.shape[0]
    batch_count = lax.axis_size("batch")
    low_count = 1
    while (2 * low_count) ** 2 <= batch_count:
        low_count *= 2
    high_count = batch_count // low_count
    members = 2 * low_count
    columns = high_count * half
    vmem = pl.BlockSpec(memory_space=pltpu.VMEM)
    smem = pl.BlockSpec(memory_space=pltpu.SMEM)
    hbm = pl.BlockSpec(memory_space=pl.ANY)
    dma = pltpu.SemaphoreType.DMA

    def pair(count):
        return [dma((count,)), dma((count,))]

    loss, image_grad, text_grad = pl.pallas_call(
        functools.partial(kernel, low_count, high_count, rows * batch_count),
        out_shape=(
            jax.ShapeDtypeStruct((1, 1), F32),
            jax.ShapeDtypeStruct((half, width), F32),
            jax.ShapeDtypeStruct((half, width), F32),
        ),
        in_specs=[smem, hbm, hbm],
        out_specs=(smem, vmem, vmem),
        scratch_shapes=[
            pltpu.VMEM((low_count, rows, width), BF16),
            pltpu.VMEM((columns, width), BF16),
            pltpu.VMEM((low_count, rows, columns), F32),
            pltpu.VMEM((low_count * rows, columns), BF16),
            pltpu.VMEM((members, 4, low_count * rows), F32),
            pltpu.VMEM((high_count, 4, columns), F32),
            pltpu.VMEM((high_count, 1, 128), F32),
            pltpu.VMEM((members, 1, 128), F32),
            pltpu.VMEM((members, half, width), BF16),
            pltpu.VMEM((high_count, half, width), BF16),
            pltpu.VMEM((members, half, width), BF16),
            pltpu.VMEM((high_count, half, width), BF16),
            pltpu.VMEM((half, width), F32),
            pltpu.VMEM((half, width), F32),
            dma((2,)),
        ]
        + pair(low_count)
        + pair(high_count)
        + pair(members)
        + pair(high_count)
        + pair(high_count)
        + pair(members)
        + pair(members)
        + pair(high_count),
        compiler_params=pltpu.CompilerParams(
            collective_id=0, has_side_effects=True, vmem_limit_bytes=60 * 1024 * 1024
        ),
    )(logit_scale, image_embed, text_embed)
    return (loss.reshape(()), image_grad, text_grad)


def solution(mesh):
    in_specs = (P("batch", None), P(("batch", "rep"), None), P())
    out_specs = (P(), P(("batch", "rep"), None), P(("batch", "rep"), None))
    return jax.shard_map(body, mesh=mesh, in_specs=in_specs, out_specs=out_specs, check_vma=False)
```

time: 189 us -> 45 us (0.24)
  the two profiles are of different devices: /device:TPU:0 before, /device:TPU:1 now
where the time goes in v1:
time: 45 us; the launch traced here: 44.9 us
  Pallas kernels  39.4 us (88%)
  between operations  3.06 us (7%)
  local copies, waits for them, and re-layouts  2.42 us (5%)
    pallas_call x1, Pallas kernels, body(): pl.pallas_call(functools.partial(kernel, low_count, high_count, rows * ba...  39.4 us
    unnamed x4, local copies, waits for them, and re-layouts  2.42 us

profile of v1, /device:TPU:1, one launch (start us, length us, event | category | flops | bytes accessed | tf_op | source)
XLA Modules:
  0.0 44.9 jit_solution(18144727537948452886)
XLA Ops:
  1.3 39.4 %shard_map.58 = (f32[1,1]{1,0:T(1,128)}, f32[64,1024]{1,0:T(8,128)}, f32[64,1024]{1,0:T(8,128)}) custom-call(f32[1]{0:T(128)S(6)} %copy.9.scale_ref, bf16[128,1024]{1,0:T(8,128)(2,1)} %image_hbm.1, bf16[64,1024]{1,0:T(8,128)(2,1)} %text_hbm.1), custom_call_target="tpu_custom_call" | custom-call | tf_op jit(solution)/shard_map/pallas_call | solution.py:336
  41.3 0.0 copy-start
  41.3 1.7 %copy.11 = f32[64,1024]{1,0:T(8,128)} copy(f32[64,1024]{1,0:T(8,128)} %get-tuple-element.13) | data formatting | bytes 524288
  43.0 0.0 copy-done
  43.0 0.7 %copy.12 = f32[64,1024]{1,0:T(8,128)} copy(f32[64,1024]{1,0:T(8,128)S(1)} %copy-done) | data formatting | bytes 524288
Async XLA Ops:
  41.3 1.7 %copy-start = (f32[64,1024]{1,0:T(8,128)S(1)}, f32[64,1024]{1,0:T(8,128)}, u32[]{:S(2)}) copy-start(f32[64,1024]{1,0:T(8,128)} %get-tuple-element.14) | copy-start | bytes 786436

commit v2 on v1

--- a/solution.py
+++ b/solution.py
@@ -44,6 +44,10 @@
     text_in,
     image_own,
     text_own,
+    text_held,
+    text_relay,
+    core_out,
+    core_in,
     local_sems,
     image_send,
     image_recv,
@@ -61,6 +65,9 @@
     image_out_recv,
     text_out_send,
     text_out_recv,
+    core_send,
+    core_recv,
+    relay_recv,
 ):
     rows = images.shape[1]
     half = rows // 2
@@ -71,7 +78,10 @@
     low = lax.rem(batch, low_count)
     member = low * 2 + rep
     member_count = 2 * low_count
+    core = lax.rem(low, 2)
+    place = low // 2 * 2 + rep
     scale = scale_ref[0]
+    via = {3: (0, 1), 0: (3, 2)} if high_count == 4 else {}
 
     def row_device(index):
         return (high * low_count + index // 2, jnp.int32(index % 2))
@@ -144,8 +154,22 @@
 
     def image_out_copy(index):
         return remote(
-            image_out.at[index], image_in.at[member], image_out_send.at[index],
-            image_out_recv.at[member], row_device(index),
+            image_out.at[index], image_in.at[place], image_out_send.at[index],
+            image_out_recv.at[place],
+            (high * low_count + index // 2 * 2 + core, jnp.int32(index % 2)),
+        )
+
+    def core_copy(chip):
+        pieces = pl.ds(2 * chip, 2)
+        return remote(
+            core_out.at[pieces], core_in.at[pieces], core_send.at[chip], core_recv.at[chip],
+            (batch + 1 - 2 * core, rep),
+        )
+
+    def relay_copy(index, middle):
+        return remote(
+            text_out.at[index], text_relay, text_out_send.at[index], relay_recv.at[0],
+            column_device(middle),
         )
 
     def text_out_copy(index):
@@ -180,6 +204,7 @@
         return in_diag & (row_iota - diag_start == column_iota) & (low == index)
 
     lanes = lax.broadcasted_iota(jnp.int32, (rows, 128), 1)
+    span = low_count * rows
     column_max = None
     diag_sum = jnp.zeros((1, columns), F32)
     for index in range(low_count):
@@ -193,7 +218,9 @@
         row_max = jnp.max(block, axis=1, keepdims=True)
         row_sum = jnp.sum(jnp.exp(block - row_max), axis=1, keepdims=True)
         packed = jnp.where(lanes == 0, row_max, row_sum).T
-        row_stats[member, 0:2, index * rows : (index + 1) * rows] = packed[0:2]
+        here = index * rows
+        row_stats[member, 0:1, here : here + rows] = packed[0:1]
+        row_stats[member, 0:1, span + here : span + here + rows] = packed[1:2]
         block_max = jnp.max(block, axis=0, keepdims=True)
         new_max = block_max if column_max is None else jnp.maximum(column_max, block_max)
         block_sum = jnp.sum(jnp.exp(block - new_max), axis=0, keepdims=True)
@@ -205,43 +232,54 @@
         diag_sum = diag_sum + jnp.sum(
             jnp.where(diag_of(index), block, 0.0), axis=0, keepdims=True
         )
-    row_stats[member, 2:3, :] = jnp.full((1, low_count * rows), jnp.sum(diag_sum), F32)
-    column_stats[high, 0:1, :] = column_max
-    column_stats[high, 1:2, :] = column_sum
+    row_stats[member, 0:1, 2 * span :] = jnp.full((1, 128), jnp.sum(diag_sum), F32)
+    column_stats[high, 0:1, 0:columns] = column_max
+    column_stats[high, 0:1, columns:] = column_sum
     each(high_count, high, lambda index: column_copy(index).start())
     each(member_count, member, lambda index: row_copy(index).start())
 
-    def merged(stats, count):
-        top = stats[0, 0:1, :]
+    def merged(stats, count, size):
+        top = stats[0, 0:1, 0:size]
         for index in range(1, count):
-            top = jnp.maximum(top, stats[index, 0:1, :])
+            top = jnp.maximum(top, stats[index, 0:1, 0:size])
         total = jnp.zeros_like(top)
         for index in range(count):
-            total = total + stats[index, 1:2, :] * jnp.exp(stats[index, 0:1, :] - top)
+            total = total + stats[index, 0:1, size : 2 * size] * jnp.exp(
+                stats[index, 0:1, 0:size] - top
+            )
         return top + jnp.log(total)
 
     each(member_count, member, lambda index: arrived(row_stats.at[index], row_recv, index))
-    row_lse = merged(row_stats, member_count)
+    row_lse = merged(row_stats, member_count, span)
     each(high_count, high, lambda index: arrived(column_stats.at[index], column_recv, index))
-    column_lse = merged(column_stats, high_count)
-
-    diag_total = row_stats[0, 2:3, 0:128]
+    column_lse = merged(column_stats, high_count, columns)
+
+    diag_total = row_stats[0, 0:1, 2 * span :]
     for index in range(1, member_count):
-        diag_total = diag_total + row_stats[index, 2:3, 0:128]
+        diag_total = diag_total + row_stats[index, 0:1, 2 * span :]
     row_loss[high] = jnp.full((1, 128), jnp.sum(row_lse), F32) - 2.0 * diag_total
     column_loss[member] = jnp.full((1, 128), jnp.sum(column_lse), F32)
     each(high_count, high, lambda index: row_loss_copy(index).start())
     each(member_count, member, lambda index: column_loss_copy(index).start())
 
     for index in range(low_count):
-        span = pl.ds(index * rows, rows)
         block = scores[index]
         spread = jnp.broadcast_to(row_lse[:, index * rows : (index + 1) * rows], (128, rows)).T
-        weights[span] = (
+        weights[pl.ds(index * rows, rows)] = (
             jnp.exp(block - spread[:, 0:1])
             + jnp.exp(block - column_lse)
             - jnp.where(diag_of(index), 2.0, 0.0)
         ).astype(BF16)
+
+    def image_part(low_index):
+        first = pl.multiple_of(low_index * rows, rows)
+        return jnp.dot(weights[pl.ds(first, rows)], texts[...], preferred_element_type=F32)
+
+    for chip in range(low_count // 2):
+        part = image_part(2 * chip + 1 - core)
+        core_out[2 * chip] = part[:half].astype(BF16)
+        core_out[2 * chip + 1] = part[half:].astype(BF16)
+        core_copy(chip).start()
 
     per_dot = 128 // half
     for start in range(0, high_count, per_dot):
@@ -254,30 +292,56 @@
             piece = part[offset * half : (offset + 1) * half]
             text_out[index] = piece.astype(BF16)
 
-            @pl.when(index != high)
-            def _():
-                text_out_copy(index).start()
-
             @pl.when(index == high)
             def _():
                 text_own[...] = piece
 
-    for low_index in range(low_count):
-        part = jnp.dot(
-            weights[pl.ds(low_index * rows, rows)], texts[...], preferred_element_type=F32
-        )
+            if index in via:
+
+                @pl.when(high == via[index][1])
+                def _():
+                    text_held[...] = piece
+
+    for index, (origin, middle) in via.items():
+
+        @pl.when(high == origin)
+        def _():
+            relay_copy(index, middle).start()
+
+    def direct(index):
+        if index not in via:
+            text_out_copy(index).start()
+            return
+
+        @pl.when((high != via[index][0]) & (high != via[index][1]))
+        def _():
+            text_out_copy(index).start()
+
+    each(high_count, high, direct)
+
+    for chip in range(low_count // 2):
+        part = image_part(2 * chip + core)
+        arrived(core_in.at[pl.ds(2 * chip, 2)], core_recv, chip)
         for offset in range(2):
-            index = 2 * low_index + offset
-            piece = part[offset * half : (offset + 1) * half]
+            index = 2 * chip + offset
+            piece = part[offset * half : (offset + 1) * half] + core_in[index].astype(F32)
             image_out[index] = piece.astype(BF16)
 
-            @pl.when(index != member)
+            @pl.when(index != place)
             def _():
                 image_out_copy(index).start()
 
-            @pl.when(index == member)
+            @pl.when(index == place)
             def _():
                 image_own[...] = piece
+
+    for index, (origin, middle) in via.items():
+
+        @pl.when(high == middle)
+        def _():
+            arrived(text_relay, relay_recv, 0)
+            text_out[index] = (text_held[...] + text_relay[...].astype(F32)).astype(BF16)
+            text_out_copy(index).start()
 
     each(high_count, high, lambda index: arrived(row_loss.at[index], row_loss_recv, index))
     each(
@@ -290,17 +354,27 @@
         total = total + column_loss[index]
     loss_ref[0, 0] = jnp.max(total) / (2 * pair_count)
 
-    factor = scale * 0.5
-    each(high_count, high, lambda index: arrived(text_in.at[index], text_out_recv, index))
-    total = text_own[...]
-    for index in range(1, high_count):
-        total = total + text_in[lax.rem(high + index, high_count)].astype(F32)
-    text_grad_ref[...] = factor * total
-    each(member_count, member, lambda index: arrived(image_in.at[index], image_out_recv, index))
+    def text_add(index):
+        arrived(text_in.at[index], text_out_recv, index)
+        text_own[...] += text_in[index].astype(F32)
+
+    def text_join(index):
+        senders = [entry[0] for target, entry in via.items() if high_count - 1 - index == target]
+        if not senders or senders[0] != index:
+            text_add(index)
+            return
+
+        @pl.when(high != high_count - 1 - index)
+        def _():
+            text_add(index)
+
+    each(low_count, place, lambda index: arrived(image_in.at[index], image_out_recv, index))
     total = image_own[...]
-    for index in range(1, member_count):
-        total = total + image_in[lax.rem(member + index, member_count)].astype(F32)
-    image_grad_ref[...] = factor * total
+    for index in range(1, low_count):
+        total = total + image_in[lax.rem(place + index, low_count)].astype(F32)
+    image_grad_ref[...] = total
+    each(high_count, high, text_join)
+    text_grad_ref[...] = text_own[...]
 
     for count, own, copy in (
         (low_count, low, image_copy),
@@ -309,10 +383,12 @@
         (high_count, high, column_copy),
         (high_count, high, row_loss_copy),
         (member_count, member, column_loss_copy),
-        (member_count, member, image_out_copy),
+        (low_count, place, image_out_copy),
         (high_count, high, text_out_copy),
     ):
         each(count, own, lambda index: copy(index).wait_send())
+    for chip in range(low_count // 2):
+        core_copy(chip).wait_send()
 
 
 def body(image_embed, text_embed, logit_scale):
@@ -347,16 +423,20 @@
             pltpu.VMEM((columns, width), BF16),
             pltpu.VMEM((low_count, rows, columns), F32),
             pltpu.VMEM((low_count * rows, columns), BF16),
-            pltpu.VMEM((members, 4, low_count * rows), F32),
-            pltpu.VMEM((high_count, 4, columns), F32),
+            pltpu.VMEM((members, 1, 2 * low_count * rows + 128), F32),
+            pltpu.VMEM((high_count, 1, 2 * columns), F32),
             pltpu.VMEM((high_count, 1, 128), F32),
             pltpu.VMEM((members, 1, 128), F32),
-            pltpu.VMEM((members, half, width), BF16),
+            pltpu.VMEM((low_count, half, width), BF16),
             pltpu.VMEM((high_count, half, width), BF16),
-            pltpu.VMEM((members, half, width), BF16),
+            pltpu.VMEM((low_count, half, width), BF16),
             pltpu.VMEM((high_count, half, width), BF16),
             pltpu.VMEM((half, width), F32),
             pltpu.VMEM((half, width), F32),
+            pltpu.VMEM((half, width), F32),
+            pltpu.VMEM((half, width), BF16),
+            pltpu.VMEM((low_count, half, width), BF16),
+            pltpu.VMEM((low_count, half, width), BF16),
             dma((2,)),
         ]
         + pair(low_count)
@@ -365,13 +445,16 @@
         + pair(high_count)
         + pair(high_count)
         + pair(members)
-        + pair(members)
-        + pair(high_count),
+        + pair(low_count)
+        + pair(high_count)
+        + pair(low_count // 2)
+        + [dma((1,))],
         compiler_params=pltpu.CompilerParams(
             collective_id=0, has_side_effects=True, vmem_limit_bytes=60 * 1024 * 1024
         ),
     )(logit_scale, image_embed, text_embed)
-    return (loss.reshape(()), image_grad, text_grad)
+    factor = logit_scale[0] * 0.5
+    return (loss.reshape(()), factor * image_grad, factor * text_grad)
 
 
 def solution(mesh):

time: 45 us -> 44 us (0.978)
  the two profiles are of different devices: /device:TPU:1 before, /device:TPU:0 now
where the time goes in v2:
time: 44 us; the launch traced here: 43.9 us
  Pallas kernels  38.9 us (88%)
  between operations  3.05 us (7%)
  other arithmetic  1.87 us (4%)
    pallas_call x1, Pallas kernels, body(): pl.pallas_call(functools.partial(kernel, low_count, high_count, rows * ba...  38.9 us
    mul x1, other arithmetic, body(): return (loss.reshape(()), factor * image_grad, factor * text_grad)  1.87 us

profile of v2, /device:TPU:0, one launch (start us, length us, event | category | flops | bytes accessed | tf_op | source)
XLA Modules:
  0.0 43.9 jit_solution(2643350622939806171)
XLA Ops:
  1.3 38.9 %shard_map.58 = (f32[1,1]{1,0:T(1,128)}, f32[64,1024]{1,0:T(8,128)}, f32[64,1024]{1,0:T(8,128)}) custom-call(f32[1]{0:T(128)S(6)} %copy.7.scale_ref, bf16[128,1024]{1,0:T(8,128)(2,1)} %image_hbm.1, bf16[64,1024]{1,0:T(8,128)(2,1)} %text_hbm.1), custom_call_target="tpu_custom_call" | custom-call | tf_op jit(solution)/shard_map/pallas_call | solution.py:412
  40.2 1.9 %broadcast_multiply_fusion = (f32[64,1024]{1,0:T(8,128)}, f32[64,1024]{1,0:T(8,128)}) fusion(f32[64,1024]{1,0:T(8,128)} %get-tuple-element.8, f32[]{:T(128)} %bitcast.1, f32[64,1024]{1,0:T(8,128)} %get-tuple-element.7), kind=kLoop, calls=%fused_computation | loop fusion | flops 131072 | bytes 1048580 | tf_op jit(solution)/shard_map/mul | solution.py:457

commit v3 on v2

--- a/solution.py
+++ b/solution.py
@@ -44,8 +44,7 @@
     text_in,
     image_own,
     text_own,
-    text_held,
-    text_relay,
+    column_lses,
     core_out,
     core_in,
     local_sems,
@@ -67,7 +66,6 @@
     text_out_recv,
     core_send,
     core_recv,
-    relay_recv,
 ):
     rows = images.shape[1]
     half = rows // 2
@@ -81,7 +79,12 @@
     core = lax.rem(low, 2)
     place = low // 2 * 2 + rep
     scale = scale_ref[0]
-    via = {3: (0, 1), 0: (3, 2)} if high_count == 4 else {}
+
+    group_width = 128
+    per_group = group_width // half
+    group_count = high_count // per_group
+    own_group = high // per_group
+    groups = [lax.rem(own_group + step, group_count) for step in range(group_count)]
 
     def row_device(index):
         return (high * low_count + index // 2, jnp.int32(index % 2))
@@ -121,12 +124,19 @@
         )
 
     def text_slot(index):
-        return texts.at[pl.ds(index * half, half)]
-
-    def image_copy(index):
-        return remote(
-            images.at[low], images.at[low], image_send.at[index], image_recv.at[low],
-            (high * low_count + index, rep),
+        return texts.at[pl.ds(pl.multiple_of(index * half, half), half)]
+
+    def image_copy(chip):
+        return remote(
+            images.at[low], images.at[low], image_send.at[2 * chip + core], image_recv.at[low],
+            (high * low_count + 2 * chip + core, rep),
+        )
+
+    def image_forward(chip):
+        slot = 2 * chip + core
+        return remote(
+            images.at[slot], images.at[slot], image_send.at[2 * chip + 1 - core],
+            image_recv.at[slot], (batch + 1 - 2 * core, rep),
         )
 
     def text_copy(index):
@@ -166,12 +176,6 @@
             (batch + 1 - 2 * core, rep),
         )
 
-    def relay_copy(index, middle):
-        return remote(
-            text_out.at[index], text_relay, text_out_send.at[index], relay_recv.at[0],
-            column_device(middle),
-        )
-
     def text_out_copy(index):
         return remote(
             text_out.at[index], text_in.at[high], text_out_send.at[index],
@@ -188,53 +192,77 @@
             def _():
                 action(index)
 
+    def group_members(step, action):
+        for offset in range(per_group):
+            index = groups[step] * per_group + offset
+
+            @pl.when(index != high)
+            def _():
+                action(index)
+
     text_load.wait()
-    each(high_count, high, lambda index: text_copy(index).start())
+    for step in [*range(1, group_count), 0]:
+        group_members(step, lambda index: text_copy(index).start())
     image_load.wait()
-    each(low_count, low, lambda index: image_copy(index).start())
-
-    each(high_count, high, lambda index: arrived(text_slot(index), text_recv, index))
+    chips = low_count // 2
+    own_chip = low // 2
+    each(chips, own_chip, lambda chip: image_copy(chip).start())
+    image_forward(own_chip).start()
+
+    def forward(chip):
+        arrived(images.at[2 * chip + core], image_recv, 2 * chip + core)
+        image_forward(chip).start()
+
+    each(chips, own_chip, forward)
+    for chip in range(chips):
+        arrived(images.at[2 * chip + 1 - core], image_recv, 2 * chip + 1 - core)
 
     diag_start = rep * half
-    row_iota = lax.broadcasted_iota(jnp.int32, (rows, columns), 0)
-    column_iota = lax.broadcasted_iota(jnp.int32, (rows, columns), 1) - high * half
+    row_iota = lax.broadcasted_iota(jnp.int32, (rows, group_width), 0)
+    column_iota = lax.broadcasted_iota(jnp.int32, (rows, group_width), 1)
+    column_iota = column_iota - lax.rem(high, per_group) * half
     in_diag = (column_iota >= 0) & (column_iota < half)
 
     def diag_of(index):
         return in_diag & (row_iota - diag_start == column_iota) & (low == index)
 
+    def lanes_of(step, base=0):
+        return pl.ds(pl.multiple_of(base + groups[step] * group_width, group_width), group_width)
+
     lanes = lax.broadcasted_iota(jnp.int32, (rows, 128), 1)
     span = low_count * rows
-    column_max = None
-    diag_sum = jnp.zeros((1, columns), F32)
+    row_max = [None] * low_count
+    row_sum = [None] * low_count
+    diag_sum = jnp.zeros((1, group_width), F32)
+    for step in range(group_count):
+        group_members(step, lambda index: arrived(text_slot(index), text_recv, index))
+        blocks = []
+        for index in range(low_count):
+            block = scale * nt_dot(images[index], texts[lanes_of(step)])
+            scores[groups[step], index] = block
+            blocks.append(block)
+            new_max = jnp.max(block, axis=1, keepdims=True)
+            if step > 0:
+                new_max = jnp.maximum(new_max, row_max[index])
+            new_sum = jnp.sum(jnp.exp(block - new_max), axis=1, keepdims=True)
+            if step > 0:
+                new_sum = new_sum + row_sum[index] * jnp.exp(row_max[index] - new_max)
+            row_max[index], row_sum[index] = new_max, new_sum
+            if step == 0:
+                diag_sum = diag_sum + jnp.sum(
+                    jnp.where(diag_of(index), block, 0.0), axis=0, keepdims=True
+                )
+        tops = [jnp.max(block, axis=0, keepdims=True) for block in blocks]
+        top = functools.reduce(jnp.maximum, tops)
+        sums = [jnp.sum(jnp.exp(block - top), axis=0, keepdims=True) for block in blocks]
+        column_stats[high, 0:1, lanes_of(step)] = top
+        column_stats[high, 0:1, lanes_of(step, columns)] = sum(sums[1:], sums[0])
     for index in range(low_count):
-
-        @pl.when(index != low)
-        def _():
-            arrived(images.at[index], image_recv, index)
-
-        block = scale * nt_dot(images[index], texts[...])
-        scores[index] = block
-        row_max = jnp.max(block, axis=1, keepdims=True)
-        row_sum = jnp.sum(jnp.exp(block - row_max), axis=1, keepdims=True)
-        packed = jnp.where(lanes == 0, row_max, row_sum).T
+        packed = jnp.where(lanes == 0, row_max[index], row_sum[index]).T
         here = index * rows
         row_stats[member, 0:1, here : here + rows] = packed[0:1]
         row_stats[member, 0:1, span + here : span + here + rows] = packed[1:2]
-        block_max = jnp.max(block, axis=0, keepdims=True)
-        new_max = block_max if column_max is None else jnp.maximum(column_max, block_max)
-        block_sum = jnp.sum(jnp.exp(block - new_max), axis=0, keepdims=True)
-        if column_max is None:
-            column_sum = block_sum
-        else:
-            column_sum = column_sum * jnp.exp(column_max - new_max) + block_sum
-        column_max = new_max
-        diag_sum = diag_sum + jnp.sum(
-            jnp.where(diag_of(index), block, 0.0), axis=0, keepdims=True
-        )
     row_stats[member, 0:1, 2 * span :] = jnp.full((1, 128), jnp.sum(diag_sum), F32)
-    column_stats[high, 0:1, 0:columns] = column_max
-    column_stats[high, 0:1, columns:] = column_sum
     each(high_count, high, lambda index: column_copy(index).start())
     each(member_count, member, lambda index: row_copy(index).start())
 
@@ -262,14 +290,34 @@
     each(high_count, high, lambda index: row_loss_copy(index).start())
     each(member_count, member, lambda index: column_loss_copy(index).start())
 
-    for index in range(low_count):
-        block = scores[index]
-        spread = jnp.broadcast_to(row_lse[:, index * rows : (index + 1) * rows], (128, rows)).T
-        weights[pl.ds(index * rows, rows)] = (
-            jnp.exp(block - spread[:, 0:1])
-            + jnp.exp(block - column_lse)
-            - jnp.where(diag_of(index), 2.0, 0.0)
-        ).astype(BF16)
+    column_lses[...] = column_lse
+    spread = [
+        jnp.broadcast_to(row_lse[:, index * rows : (index + 1) * rows], (128, rows)).T
+        for index in range(low_count)
+    ]
+    for step in [*range(1, group_count), 0]:
+        here = lanes_of(step)
+        for index in range(low_count):
+            block = scores[groups[step], index]
+            value = jnp.exp(block - spread[index][:, 0:1]) + jnp.exp(block - column_lses[:, here])
+            if step == 0:
+                value = value - jnp.where(diag_of(index), 2.0, 0.0)
+            weights[pl.ds(index * rows, rows), here] = value.astype(BF16)
+        part = tn_dot(weights[:, here], images[...].reshape(span, images.shape[2]))
+        for offset in range(per_group):
+            index = groups[step] * per_group + offset
+            piece = part[offset * half : (offset + 1) * half]
+            text_out[index] = piece.astype(BF16)
+
+            @pl.when(index != high)
+            def _():
+                text_out_copy(index).start()
+
+            if step == 0:
+
+                @pl.when(index == high)
+                def _():
+                    text_own[...] = piece
 
     def image_part(low_index):
         first = pl.multiple_of(low_index * rows, rows)
@@ -280,44 +328,6 @@
         core_out[2 * chip] = part[:half].astype(BF16)
         core_out[2 * chip + 1] = part[half:].astype(BF16)
         core_copy(chip).start()
-
-    per_dot = 128 // half
-    for start in range(0, high_count, per_dot):
-        part = tn_dot(
-            weights[:, start * half : (start + per_dot) * half],
-            images[...].reshape(low_count * rows, images.shape[2]),
-        )
-        for offset in range(per_dot):
-            index = start + offset
-            piece = part[offset * half : (offset + 1) * half]
-            text_out[index] = piece.astype(BF16)
-
-            @pl.when(index == high)
-            def _():
-                text_own[...] = piece
-
-            if index in via:
-
-                @pl.when(high == via[index][1])
-                def _():
-                    text_held[...] = piece
-
-    for index, (origin, middle) in via.items():
-
-        @pl.when(high == origin)
-        def _():
-            relay_copy(index, middle).start()
-
-    def direct(index):
-        if index not in via:
-            text_out_copy(index).start()
-            return
-
-        @pl.when((high != via[index][0]) & (high != via[index][1]))
-        def _():
-            text_out_copy(index).start()
-
-    each(high_count, high, direct)
 
     for chip in range(low_count // 2):
         part = image_part(2 * chip + core)
@@ -334,14 +344,6 @@
             @pl.when(index == place)
             def _():
                 image_own[...] = piece
-
-    for index, (origin, middle) in via.items():
-
-        @pl.when(high == middle)
-        def _():
-            arrived(text_relay, relay_recv, 0)
-            text_out[index] = (text_held[...] + text_relay[...].astype(F32)).astype(BF16)
-            text_out_copy(index).start()
 
     each(high_count, high, lambda index: arrived(row_loss.at[index], row_loss_recv, index))
     each(
@@ -358,26 +360,16 @@
         arrived(text_in.at[index], text_out_recv, index)
         text_own[...] += text_in[index].astype(F32)
 
-    def text_join(index):
-        senders = [entry[0] for target, entry in via.items() if high_count - 1 - index == target]
-        if not senders or senders[0] != index:
-            text_add(index)
-            return
-
-        @pl.when(high != high_count - 1 - index)
-        def _():
-            text_add(index)
-
     each(low_count, place, lambda index: arrived(image_in.at[index], image_out_recv, index))
     total = image_own[...]
     for index in range(1, low_count):
         total = total + image_in[lax.rem(place + index, low_count)].astype(F32)
     image_grad_ref[...] = total
-    each(high_count, high, text_join)
+    each(high_count, high, text_add)
     text_grad_ref[...] = text_own[...]
 
     for count, own, copy in (
-        (low_count, low, image_copy),
+        (chips, own_chip, image_copy),
         (high_count, high, text_copy),
         (member_count, member, row_copy),
         (high_count, high, column_copy),
@@ -389,6 +381,7 @@
         each(count, own, lambda index: copy(index).wait_send())
     for chip in range(low_count // 2):
         core_copy(chip).wait_send()
+        image_forward(chip).wait_send()
 
 
 def body(image_embed, text_embed, logit_scale):
@@ -421,7 +414,7 @@
         scratch_shapes=[
             pltpu.VMEM((low_count, rows, width), BF16),
             pltpu.VMEM((columns, width), BF16),
-            pltpu.VMEM((low_count, rows, columns), F32),
+            pltpu.VMEM((columns // 128, low_count, rows, 128), F32),
             pltpu.VMEM((low_count * rows, columns), BF16),
             pltpu.VMEM((members, 1, 2 * low_count * rows + 128), F32),
             pltpu.VMEM((high_count, 1, 2 * columns), F32),
@@ -433,8 +426,7 @@
             pltpu.VMEM((high_count, half, width), BF16),
             pltpu.VMEM((half, width), F32),
             pltpu.VMEM((half, width), F32),
-            pltpu.VMEM((half, width), F32),
-            pltpu.VMEM((half, width), BF16),
+            pltpu.VMEM((1, columns), F32),
             pltpu.VMEM((low_count, half, width), BF16),
             pltpu.VMEM((low_count, half, width), BF16),
             dma((2,)),
@@ -447,8 +439,7 @@
         + pair(members)
         + pair(low_count)
         + pair(high_count)
-        + pair(low_count // 2)
-        + [dma((1,))],
+        + pair(low_count // 2),
         compiler_params=pltpu.CompilerParams(
             collective_id=0, has_side_effects=True, vmem_limit_bytes=60 * 1024 * 1024
         ),

time: 44 us -> 40 us (0.909)
  Pallas kernels: 38.9 us -> 34.9 us
    pallas_call x1, Pallas kernels: 38.9 us -> 34.9 us  [body(): pl.pallas_call(functools.partial(kernel, low_count, high_count, rows * ba...]
where the time goes in v3:
time: 40 us; the launch traced here: 39.9 us
  Pallas kernels  34.9 us (87%)
  between operations  3.05 us (8%)
  other arithmetic  1.87 us (5%)
    pallas_call x1, Pallas kernels, body(): pl.pallas_call(functools.partial(kernel, low_count, high_count, rows * ba...  34.9 us
    mul x1, other arithmetic, body(): return (loss.reshape(()), factor * image_grad, factor * text_grad)  1.87 us

profile of v3, /device:TPU:0, one launch (start us, length us, event | category | flops | bytes accessed | tf_op | source)
XLA Modules:
  0.0 39.9 jit_solution(6159373801608141223)
XLA Ops:
  1.3 34.9 %shard_map.58 = (f32[1,1]{1,0:T(1,128)}, f32[64,1024]{1,0:T(8,128)}, f32[64,1024]{1,0:T(8,128)}) custom-call(f32[1]{0:T(128)S(6)} %copy.7.scale_ref, bf16[128,1024]{1,0:T(8,128)(2,1)} %image_hbm.1, bf16[64,1024]{1,0:T(8,128)(2,1)} %text_hbm.1), custom_call_target="tpu_custom_call" | custom-call | tf_op jit(solution)/shard_map/pallas_call | solution.py:405
  36.2 1.9 %broadcast_multiply_fusion = (f32[64,1024]{1,0:T(8,128)}, f32[64,1024]{1,0:T(8,128)}) fusion(f32[64,1024]{1,0:T(8,128)} %get-tuple-element.8, f32[]{:T(128)} %bitcast.1, f32[64,1024]{1,0:T(8,128)} %get-tuple-element.7), kind=kLoop, calls=%fused_computation | loop fusion | flops 131072 | bytes 1048580 | tf_op jit(solution)/shard_map/mul | solution.py:448

commit v4 on v3

--- a/solution.py
+++ b/solution.py
@@ -28,8 +28,7 @@
     image_hbm,
     text_hbm,
     loss_ref,
-    image_grad_ref,
-    text_grad_ref,
+    grads_ref,
     images,
     texts,
     scores,
@@ -295,6 +294,24 @@
         jnp.broadcast_to(row_lse[:, index * rows : (index + 1) * rows], (128, rows)).T
         for index in range(low_count)
     ]
+    def text_part(step):
+        here = lanes_of(step)
+        part = tn_dot(weights[:, here], images[...].reshape(span, images.shape[2]))
+        for offset in range(per_group):
+            index = groups[step] * per_group + offset
+            piece = part[offset * half : (offset + 1) * half]
+            text_out[index] = piece.astype(BF16)
+
+            @pl.when(index != high)
+            def _():
+                text_out_copy(index).start()
+
+            if step == 0:
+
+                @pl.when(index == high)
+                def _():
+                    text_own[...] = piece
+
     for step in [*range(1, group_count), 0]:
         here = lanes_of(step)
         for index in range(low_count):
@@ -303,21 +320,8 @@
             if step == 0:
                 value = value - jnp.where(diag_of(index), 2.0, 0.0)
             weights[pl.ds(index * rows, rows), here] = value.astype(BF16)
-        part = tn_dot(weights[:, here], images[...].reshape(span, images.shape[2]))
-        for offset in range(per_group):
-            index = groups[step] * per_group + offset
-            piece = part[offset * half : (offset + 1) * half]
-            text_out[index] = piece.astype(BF16)
-
-            @pl.when(index != high)
-            def _():
-                text_out_copy(index).start()
-
-            if step == 0:
-
-                @pl.when(index == high)
-                def _():
-                    text_own[...] = piece
+        if step > 0:
+            text_part(step)
 
     def image_part(low_index):
         first = pl.multiple_of(low_index * rows, rows)
@@ -328,6 +332,8 @@
         core_out[2 * chip] = part[:half].astype(BF16)
         core_out[2 * chip + 1] = part[half:].astype(BF16)
         core_copy(chip).start()
+
+    text_part(0)
 
     for chip in range(low_count // 2):
         part = image_part(2 * chip + core)
@@ -364,9 +370,9 @@
     total = image_own[...]
     for index in range(1, low_count):
         total = total + image_in[lax.rem(place + index, low_count)].astype(F32)
-    image_grad_ref[...] = total
+    grads_ref[0] = total
     each(high_count, high, text_add)
-    text_grad_ref[...] = text_own[...]
+    grads_ref[1] = text_own[...]
 
     for count, own, copy in (
         (chips, own_chip, image_copy),
@@ -402,15 +408,14 @@
     def pair(count):
         return [dma((count,)), dma((count,))]
 
-    loss, image_grad, text_grad = pl.pallas_call(
+    loss, grads = pl.pallas_call(
         functools.partial(kernel, low_count, high_count, rows * batch_count),
         out_shape=(
             jax.ShapeDtypeStruct((1, 1), F32),
-            jax.ShapeDtypeStruct((half, width), F32),
-            jax.ShapeDtypeStruct((half, width), F32),
+            jax.ShapeDtypeStruct((2, half, width), F32),
         ),
         in_specs=[smem, hbm, hbm],
-        out_specs=(smem, vmem, vmem),
+        out_specs=(smem, vmem),
         scratch_shapes=[
             pltpu.VMEM((low_count, rows, width), BF16),
             pltpu.VMEM((columns, width), BF16),
@@ -445,7 +450,7 @@
         ),
     )(logit_scale, image_embed, text_embed)
     factor = logit_scale[0] * 0.5
-    return (loss.reshape(()), factor * image_grad, factor * text_grad)
+    return (loss.reshape(()), factor * grads[0], factor * grads[1])
 
 
 def solution(mesh):

time: 40 us -> 40 us (level)
  no operation moved by 1% of the time
where the time goes in v4:
time: 40 us; the launch traced here: 39.9 us
  Pallas kernels  34.9 us (87%)
  between operations  3.05 us (8%)
  other arithmetic  1.87 us (5%)
    pallas_call x1, Pallas kernels, body(): pl.pallas_call(functools.partial(kernel, low_count, high_count, rows * ba...  34.9 us
    mul x1, other arithmetic, body(): return (loss.reshape(()), factor * grads[0], factor * grads[1])  1.87 us

profile of v4, /device:TPU:0, one launch (start us, length us, event | category | flops | bytes accessed | tf_op | source)
XLA Modules:
  0.0 39.9 jit_solution(1328175636257736126)
XLA Ops:
  1.3 34.9 %shard_map.58 = (f32[1,1]{1,0:T(1,128)}, f32[2,64,1024]{2,1,0:T(8,128)}) custom-call(f32[1]{0:T(128)S(6)} %copy.7.scale_ref, bf16[128,1024]{1,0:T(8,128)(2,1)} %image_hbm.1, bf16[64,1024]{1,0:T(8,128)(2,1)} %text_hbm.1), custom_call_target="tpu_custom_call" | custom-call | tf_op jit(solution)/shard_map/pallas_call | solution.py:411
  36.2 1.9 %multiply_bitcast_fusion = (f32[64,1024]{1,0:T(8,128)}, f32[64,1024]{1,0:T(8,128)}) fusion(f32[2,64,1024]{2,1,0:T(8,128)} %get-tuple-element.6, f32[]{:T(128)} %bitcast.1), kind=kLoop, calls=%fused_computation | loop fusion | flops 131072 | bytes 1048580 | tf_op jit(solution)/shard_map/mul | solution.py:453
